TPU v7x, 32 devices: a whole 2x2x4 slice. The times are simulated.
32 devices in a mesh: tp: 4 (over x, core), fsdp: 8 (over z, y).
Axes of the slice: x: 2, y: 2, z: 4, core: 2. Of those that a mesh axis runs over, the one named last changes fastest.
Arguments:
- sectioned: bfloat16 [64, 256, 26624], P('fsdp', None, 'tp'), as said below
- loader_owner: int32 [64], replicated, may hold values from 0 to 7, as said below
- slab_order: int32 [64], replicated, may hold values from 0 to 7, as said below
Outputs:
- dequant: bfloat16 [16384, 26624], P(('tp', 'fsdp'))
- scale_codes: float32 [26624, 256], P(('tp', 'fsdp'))
- group_max: float32 [26624], P(('tp', 'fsdp'))
Inputs may be any that keep to these rules, and one draw needn't show every extreme that they name: `loader_owner`: slab s holds rows s * 256 to (s + 1) * 256 - 1; for each f, the 8 slabs s with (s // 2) % 8 == f have 8 distinct owners. `slab_order`: the slabs of one owner have distinct orders. `sectioned`: entries are finite.
All inputs are finite; a program needn't handle non-finite values. Where the computation divides by a largest or mean magnitude, that divisor is 1e-20 or more.
Results may differ from a plain program's by a relative error of at most 0.0015.
Values may be sent and summed in bfloat16 or wider, within the bound.
A program may use at most 256 MiB of HBM per device.

v0:
```python
import jax
import jax.numpy as jnp
from jax import lax
from jax.sharding import PartitionSpec as P

D = 16384
FFW = 26624


LEVELS = [
    -1.0,
    -0.6961928009986877,
    -0.5250730514526367,
    -0.39491748809814453,
    -0.28444138169288635,
    -0.18477343022823334,
    -0.09105003625154495,
    0.0,
    0.07958029955625534,
    0.16093020141124725,
    0.24611230194568634,
    0.33791524171829224,
    0.44070982933044434,
    0.5626170039176941,
    0.7229568362236023,
    1.0,
]
MIDPOINTS = [(LEVELS[k] + LEVELS[k + 1]) / 2.0 for k in range(15)]
STEPSIZES = [LEVELS[k + 1] - LEVELS[k] for k in range(15)]
EPS = 1e-06


def block_absmax(block):
    values = block.astype(jnp.float32)
    shape = values.shape
    grouped = values.reshape(shape[:-1] + (shape[-1] // 64, 64))
    return jnp.max(jnp.abs(grouped), axis=-1)


def hard_code(block):
    values = block.astype(jnp.float32)
    shape = values.shape
    absmax = block_absmax(block)
    spread = jnp.repeat(absmax, 64, axis=-1)
    ratio = values / (spread + EPS)
    level = jnp.full(shape, LEVELS[0], jnp.float32)
    for middle, stepsize in zip(MIDPOINTS, STEPSIZES):
        level = level + jnp.where(ratio > middle, stepsize, 0.0).astype(jnp.float32)
    coded = (spread * level).astype(jnp.bfloat16)
    return (coded, absmax)


def per_device(sectioned, loader_owner, slab_order):
    owners = lax.axis_size("fsdp")
    tp_count = lax.axis_size("tp")
    myself = lax.axis_index("fsdp")
    slots, slab_rows, columns = sectioned.shape
    slab_count = loader_owner.shape[0]
    per_block = owners // tp_count
    shard_rows = slab_rows * per_block
    slab_ids = jnp.arange(slab_count, dtype=jnp.int32)
    target = slab_ids // per_block % owners
    held = loader_owner == myself
    picks = (target[None, :] == jnp.arange(owners, dtype=jnp.int32)[:, None]) & held[None, :]
    send_slot = jnp.sum(jnp.where(picks, slab_order[None, :], 0), axis=1)
    outgoing = jnp.take(sectioned, send_slot, axis=0)
    place = jnp.arange(owners, dtype=jnp.int32)
    wanted = (place // per_block * owners + myself) * per_block + place % per_block
    from_owner = jnp.take(loader_owner, wanted, axis=0)
    arrived = lax.all_to_all(outgoing, "fsdp", split_axis=0, concat_axis=0, tiled=True)
    arrived = jnp.take(arrived, from_owner, axis=0).reshape(tp_count, shard_rows, columns)
    joined = lax.all_to_all(arrived, "tp", split_axis=0, concat_axis=2, tiled=True)
    dequant, absmax = hard_code(joined.reshape(shard_rows, tp_count * columns))
    source_sum = jnp.sum(block_absmax(sectioned))
    total = lax.psum(source_sum, ("tp", "fsdp"))
    offset = total / float(D * FFW // 64)
    centred = absmax.reshape(-1, 256) - offset
    group_max = jnp.max(jnp.abs(centred), axis=1)
    scale_codes = centred / (group_max[:, None] + EPS)
    return (dequant, scale_codes, group_max)


def solution(mesh):
    return jax.shard_map(
        per_device,
        mesh=mesh,
        in_specs=(P("fsdp", None, "tp"), P(), P()),
        out_specs=(P(("tp", "fsdp"), None), P(("tp", "fsdp"), None), P(("tp", "fsdp"))),
        check_vma=False,
    )
```

profile of v0, /device:TPU:0, one launch (start us, length us, event | category | flops | bytes accessed | tf_op | source)
XLA Modules:
  0.0 1356.2 jit_solution(11074019058810456794)
XLA Ops:
  2.1 19.5 %fusion.15 = (bf16[8,256,3328]{2,1,0:T(8,128)(2,1)}, bf16[8,256,3328]{2,1,0:T(8,128)(2,1)}) fusion(bf16[8,256,6656]{2,1,0:T(8,128)(2,1)} %param.5), kind=kLoop, calls=%fused_computation.61 | loop fusion | bytes 54525952 | tf_op jit(solution)/shard_map/jit(_take)/gather | solution.py:66
  21.6 11.6 gather_fusion.1
  33.2 11.8 gather_fusion.2
  45.0 19.0 %maximum_select_fusion = bf16[8,256,6656]{2,1,0:T(8,128)(2,1)} fusion(bf16[8,256,3328]{2,1,0:T(8,128)(2,1)} %gather_fusion.2, bf16[8,256,3328]{2,1,0:T(8,128)(2,1)} %gather_fusion.1, pred[8]{0:T(512)(128)(4,1)S(1)} %compare_and_fusion.1), kind=kLoop, calls=%fused_computation.13 | loop fusion | flops 68157440 | bytes 54525960 | tf_op jit(solution)/shard_map/jit(_take)/select_n | solution.py:66
  64.0 7.3 all-to-all-start
  72.0 588.3 %all-to-all-done = bf16[8,256,6656]{2,1,0:T(8,128)(2,1)} async-done(((bf16[8,256,6656]{2,1,0:T(8,128)(2,1)}), bf16[8,256,6656]{2,1,0:T(8,128)(2,1)}, u32[]{:S(2)}, u32[]{:S(2)}) %all-to-all-start) | async-done | bytes 27263008 | tf_op jit(solution)/shard_map/all_to_all | solution.py:70
  660.3 19.4 %fusion.14 = (bf16[8,256,3328]{2,1,0:T(8,128)(2,1)}, bf16[8,256,3328]{2,1,0:T(8,128)(2,1)}) fusion(bf16[8,256,6656]{2,1,0:T(8,128)(2,1)} %all-to-all-done), kind=kLoop, calls=%fused_computation.60 | loop fusion | bytes 54525952 | tf_op jit(solution)/shard_map/jit(_take)/gather | solution.py:71
  679.7 11.8 gather_fusion.3
  691.4 11.7 gather_fusion.4
  703.2 19.0 %maximum_select_fusion.1 = bf16[8,256,6656]{2,1,0:T(8,128)(2,1)} fusion(bf16[8,256,3328]{2,1,0:T(8,128)(2,1)} %gather_fusion.4, bf16[8,256,3328]{2,1,0:T(8,128)(2,1)} %gather_fusion.3, pred[8]{0:T(512)(128)(4,1)S(1)} %get-tuple-element.19), kind=kLoop, calls=%fused_computation.14 | loop fusion | flops 68157440 | bytes 54525960 | tf_op jit(solution)/shard_map/jit(_take)/select_n | solution.py:71
  722.2 8.8 all-to-all-start.1
  730.9 33.3 %copy.26 = bf16[8,256,6656]{1,2,0:T(8,128)(2,1)} copy(bf16[8,256,6656]{2,1,0:T(8,128)(2,1)} %param.5) | data formatting | bytes 54525952 | tf_op args[0]
  764.2 26.0 %convert_abs_fusion.1 = f32[8,256,6656]{1,2,0:T(8,128)} fusion(bf16[8,256,6656]{1,2,0:T(8,128)(2,1)} %copy.26), kind=kLoop, calls=%fused_computation.12 | loop fusion | flops 27262976 | bytes 81788928 | tf_op jit(solution)/shard_map/abs | solution.py:37
  790.2 17.2 %reduce_max.28 = f32[8,256,104]{1,2,0:T(8,128)S(1)} reduce(f32[8,256,104,64]{1,3,2,0:T(8,128)} %bitcast.26, f32[]{:T(128)} %constant.79.clone.1), dimensions={3}, to_apply=%region_2.4 | reduce | flops 13418496 | bytes 55377924 | tf_op jit(solution)/shard_map/reduce_max | solution.py:37
  808.3 249.8 %psum.7 = f32[]{:T(128)} all-reduce(f32[]{:T(128)} %reduce_sum.19), channel_id=1, replica_groups=mesh['tp'=4,'fsdp'=8] {'tp','fsdp'}, use_global_device_ids=true, to_apply=%region_4.6 | all-reduce | flops 1 | bytes 8 | tf_op jit(solution)/shard_map/psum | solution.py:75
  1058.8 26.3 %fusion = f32[1,512,4,6656]{3,1,2,0:T(8,128)} fusion(bf16[4,512,6656]{2,1,0:T(8,128)(2,1)} %all-to-all-done.1), kind=kLoop, calls=%fused_computation.9 | loop fusion | flops 27262976 | bytes 81788928 | tf_op jit(solution)/shard_map/abs | solution.py:37
  1085.1 50.0 %copy.24 = f32[1,512,4,6656]{1,3,2,0:T(8,128)} copy(f32[1,512,4,6656]{3,1,2,0:T(8,128)} %fusion) | data formatting | bytes 109051904 | tf_op jit(solution)/shard_map/abs | solution.py:37
  1135.2 17.3 %reduce_max.27 = f32[512,416]{0,1:T(8,128)S(1)} reduce(f32[512,416,64]{0,2,1:T(8,128)} %bitcast.27, f32[]{:T(128)} %constant.79.clone.1), dimensions={2}, to_apply=%region_1.3 | reduce | flops 13418496 | bytes 55377924 | tf_op jit(solution)/shard_map/reduce_max | solution.py:37
  1152.9 0.8 sub.26
  1154.0 1.1 broadcast_divide_fusion
  1155.0 26.4 %convert_bitcast_fusion = f32[1,512,4,6656]{3,1,2,0:T(8,128)} fusion(bf16[4,512,6656]{2,1,0:T(8,128)(2,1)} %all-to-all-done.1), kind=kLoop, calls=%fused_computation.7 | loop fusion | flops 13631488 | bytes 81788928 | tf_op jit(solution)/shard_map/convert_element_type | solution.py:34
  1181.4 50.0 %copy.25 = f32[1,512,4,6656]{1,3,2,0:T(8,128)} copy(f32[1,512,4,6656]{3,1,2,0:T(8,128)} %convert_bitcast_fusion) | data formatting | bytes 109051904 | tf_op jit(solution)/shard_map/convert_element_type | solution.py:34
  1231.4 88.9 %fusion.2 = bf16[512,26624]{0,1:T(8,128)(2,1)} fusion(f32[1,512,4,6656]{1,3,2,0:T(8,128)} %copy.25, f32[512,416]{0,1:T(8,128)S(1)} %reduce_max.27), kind=kLoop, calls=%fused_computation.11 | loop fusion | flops 667942912 | bytes 82640896 | tf_op jit(solution)/shard_map/convert_element_type | solution.py:49
  1320.3 35.9 %copy.28 = bf16[512,26624]{1,0:T(8,128)(2,1)} copy(bf16[512,26624]{0,1:T(8,128)(2,1)} %fusion.2) | data formatting | bytes 54525952
  (21 shorter events, 3.6 us)
Async XLA Ops:
  45.0 26.3 %copy-start = (s32[64]{0:T(128)S(1)}, s32[64]{0:T(128)}, u32[]{:S(2)}) copy-start(s32[64]{0:T(128)} %param.6) | copy-start | bytes 772
  64.0 596.3 %all-to-all-start = ((bf16[8,256,6656]{2,1,0:T(8,128)(2,1)}), bf16[8,256,6656]{2,1,0:T(8,128)(2,1)}, u32[]{:S(2)}, u32[]{:S(2)}) async-start(bf16[8,256,6656]{2,1,0:T(8,128)(2,1)} %maximum_select_fusion), calls=%async_computation | async-start | bytes 54525952 | tf_op jit(solution)/shard_map/all_to_all | solution.py:70
  722.2 336.6 %all-to-all-start.1 = ((bf16[4,512,6656]{2,1,0:T(8,128)(2,1)}), bf16[4,512,6656]{2,1,0:T(8,128)(2,1)}, u32[]{:S(2)}, u32[]{:S(2)}) async-start(bf16[4,512,6656]{2,1,0:T(8,128)(2,1)} %bitcast.28), calls=%async_computation.1 | async-start | bytes 54525952 | tf_op jit(solution)/shard_map/all_to_all | solution.py:72
  1153.9 77.5 %copy-start.1 = (f32[832]{0:T(1024)}, f32[832]{0:T(1024)S(1)}, u32[]{:S(2)}) copy-start(f32[832]{0:T(1024)S(1)} %abs_reduce_fusion) | copy-start | bytes 9988
where the time goes:
time: 1360 us
  waiting for transfers between devices  588 us (43%)
  local copies, waits for them, and re-layouts  257 us (19%)
  blocking collectives  250 us (18%)
  other arithmetic  244 us (18%)
  starting transfers between devices  16.1 us (1%)
    all_to_all x1, waiting for transfers between devices, per_device(): lax.all_to_all(outgoing, 'fsdp', split_axis=0, concat_axis=0, tiled=True)  588 us
    psum x1, blocking collectives, per_device(): total = lax.psum(source_sum, ('tp', 'fsdp'))  250 us
    convert_element_type x1, other arithmetic, hard_code(): coded = (spread * level).astype(jnp.bfloat16)  88.9 us
    unnamed x6, local copies, waits for them, and re-layouts  69.2 us
    abs x2, other arithmetic, block_absmax(): return jnp.max(jnp.abs(grouped), axis=-1)  52.4 us
    abs x1, local copies, waits for them, and re-layouts, block_absmax(): return jnp.max(jnp.abs(grouped), axis=-1)  50 us
    convert_element_type x1, local copies, waits for them, and re-layouts, block_absmax(): values = block.astype(jnp.float32)  50 us
    gather x3, local copies, waits for them, and re-layouts, per_device(): outgoing = jnp.take(sectioned, send_slot, axis=0)  42.9 us
  transfers between devices with their start and end apart: 2, of which 1 were waited for; matrix products, arithmetic and copies ran while one was open for 6% of the time, Pallas kernels for 0%

commit v1 on v0

v1 whole, which is shorter than its diff:
```python
import functools

import jax
import jax.numpy as jnp
import numpy as np
from jax import lax
from jax.experimental import pallas as pl
from jax.experimental.pallas import tpu as pltpu
from jax.sharding import PartitionSpec as P

LEVELS = [
    -1.0,
    -0.6961928009986877,
    -0.5250730514526367,
    -0.39491748809814453,
    -0.28444138169288635,
    -0.18477343022823334,
    -0.09105003625154495,
    0.0,
    0.07958029955625534,
    0.16093020141124725,
    0.24611230194568634,
    0.33791524171829224,
    0.44070982933044434,
    0.5626170039176941,
    0.7229568362236023,
    1.0,
]
MIDPOINTS = [(LEVELS[k] + LEVELS[k + 1]) / 2.0 for k in range(15)]
STEPSIZES = [LEVELS[k + 1] - LEVELS[k] for k in range(15)]
EPS = 1e-06
LANES = 128
BLOCK = 64
MESH = pl.DeviceIdType.MESH


def reached_levels():
    total = np.float32(LEVELS[0])
    reached = [float(total)]
    for step in STEPSIZES:
        total = np.float32(total + np.float32(step))
        reached.append(float(total))
    return reached


REACHED = reached_levels()


def code_tile(w):
    lane = lax.broadcasted_iota(jnp.int32, w.shape, 1)
    top = jnp.abs(w)
    low = lane < BLOCK
    first = jnp.broadcast_to(jnp.max(jnp.where(low, top, 0.0), axis=1, keepdims=True), w.shape)
    second = jnp.broadcast_to(jnp.max(jnp.where(low, 0.0, top), axis=1, keepdims=True), w.shape)
    spread = jnp.where(lane < BLOCK, first, second)
    ratio = w / (spread + EPS)
    level = jnp.full(w.shape, REACHED[0], jnp.float32)
    for middle, value in zip(MIDPOINTS, REACHED[1:]):
        level = jnp.where(ratio > middle, value, level)
    return spread * level, first, second


def exchange(
    sizes, from_owner, outgoing, out, scales, sums, arrive, coded, tops, s1, r1, l1, s2, r2, l2, sa, ra, la,
    mine, ours, got, met, sm, rm, so, ro, stage,
):
    owners, tp, chunks, rows, per_block, columns, depth = sizes
    t = lax.axis_index("tp")
    f = lax.axis_index("fsdp")
    groups = columns // LANES
    width = next(u for u in range(13, 0, -1) if groups % u == 0)

    barrier = pltpu.get_barrier_semaphore()
    for d in range(1, owners):
        pl.semaphore_signal(barrier, inc=1, device_id={"fsdp": lax.rem(f + d, owners)}, device_id_type=MESH)
    for e in range(1, tp):
        pl.semaphore_signal(barrier, inc=1, device_id={"tp": lax.rem(t + e, tp)}, device_id_type=MESH)
    pl.semaphore_wait(barrier, owners - 1 + tp - 1)

    def span(c):
        return pl.ds(pl.multiple_of(c * rows, rows), rows)

    def first_hop(c, d):
        to = lax.rem(f + d, owners)
        return pltpu.make_async_remote_copy(
            src_ref=outgoing.at[to, span(c)],
            dst_ref=arrive.at[c, f],
            send_sem=s1.at[c, d],
            recv_sem=r1.at[c, d],
            device_id={"fsdp": to},
            device_id_type=MESH,
        )

    def first_stay(c):
        return pltpu.make_async_copy(outgoing.at[f, span(c)], arrive.at[c, f], l1.at[c])

    def start_chunk(c):
        for d in range(1, owners):
            first_hop(c, d).start()
        first_stay(c).start()

    def second_hop(c, slot, e):
        to = lax.rem(t + e, tp)
        band = pl.ds(pl.multiple_of(t * columns, LANES), columns)
        data = pltpu.make_async_remote_copy(
            src_ref=coded.at[slot, to],
            dst_ref=out.at[:, span(c), band],
            send_sem=s2.at[slot, e],
            recv_sem=r2.at[c, e],
            device_id={"tp": to},
            device_id_type=MESH,
        )
        top = pltpu.make_async_remote_copy(
            src_ref=tops.at[to, :, span(c)],
            dst_ref=scales.at[t, :, span(c)],
            send_sem=sa.at[slot, e],
            recv_sem=ra.at[c, e],
            device_id={"tp": to},
            device_id_type=MESH,
        )
        return data, top

    def second_stay(c, slot):
        band = pl.ds(pl.multiple_of(t * columns, LANES), columns)
        data = pltpu.make_async_copy(coded.at[slot, t], out.at[:, span(c), band], l2.at[slot])
        top = pltpu.make_async_copy(tops.at[t, :, span(c)], scales.at[t, :, span(c)], la.at[slot])
        return data, top

    def drain(c, slot):
        for e in range(1, tp):
            for copy in second_hop(c, slot, e):
                copy.wait_send()
        for copy in second_stay(c, slot):
            copy.wait()

    def code(c, slot, to):
        lane = lax.broadcasted_iota(jnp.int32, (rows, LANES), 1)

        def place(k, _):
            owner = from_owner[to * per_block + k]

            def step(g, held):
                at = pl.multiple_of(g * (width * LANES), width * LANES)
                w = stage[owner, :, pl.ds(at, width * LANES)].astype(jnp.float32)
                made = []
                for j in range(width):
                    value, first, second = code_tile(w[:, j * LANES : (j + 1) * LANES])
                    made.append(value.astype(jnp.bfloat16))
                    index = 2 * (g * width + j)
                    held = jnp.where(lane == index, first, jnp.where(lane == index + 1, second, held))
                coded[slot, to, k, :, pl.ds(at, width * LANES)] = jnp.concatenate(made, axis=1)
                return held

            held = lax.fori_loop(0, groups // width, step, jnp.zeros((rows, LANES), jnp.float32))
            tops[to, k, span(c), :] = held
            mine[...] += held
            return 0

        lax.fori_loop(0, per_block, place, 0)

    def sum_hop(d):
        return pltpu.make_async_remote_copy(
            src_ref=mine,
            dst_ref=got.at[d],
            send_sem=sm.at[d],
            recv_sem=rm.at[d],
            device_id={"fsdp": lax.rem(f + d, owners)},
            device_id_type=MESH,
        )

    def sum_turn(e):
        return pltpu.make_async_remote_copy(
            src_ref=ours,
            dst_ref=met.at[e],
            send_sem=so.at[e],
            recv_sem=ro.at[e],
            device_id={"tp": lax.rem(t + e, tp)},
            device_id_type=MESH,
        )

    for c in range(min(depth, chunks)):
        start_chunk(c)
    mine[...] = jnp.zeros_like(mine)

    def chunk(c, _):
        slot = lax.rem(c, 2)
        for d in range(1, owners):
            first_hop(c, d).wait_recv()
        first_stay(c).wait()

        @pl.when(c + depth < chunks)
        def _():
            start_chunk(c + depth)

        @pl.when(c >= 2)
        def _():
            drain(c - 2, slot)

        def take(o, _):
            stage[o] = arrive[c, o]
            return 0

        lax.fori_loop(0, owners, take, 0)
        for e in range(1, tp + 1):
            code(c, slot, lax.rem(t + e, tp))
            if e > 1:
                for copy in second_hop(c, slot, e - 1):
                    copy.start()
        for copy in second_stay(c, slot):
            copy.start()
        return 0

    lax.fori_loop(0, chunks, chunk, 0)

    if chunks > 1:
        drain(chunks - 2, chunks % 2)
    for d in range(1, owners):
        sum_hop(d).start()
    drain(chunks - 1, (chunks - 1) % 2)
    for d in range(1, owners):
        sum_hop(d).wait()
    total = mine[...]
    for d in range(1, owners):
        total = total + got[d]
    ours[...] = total

    def finish(c, _):
        for d in range(1, owners):
            first_hop(c, d).wait_send()
        for e in range(1, tp):
            for copy in second_hop(c, 0, e):
                copy.wait_recv()
        return 0

    lax.fori_loop(0, chunks, finish, 0)
    for e in range(1, tp):
        sum_turn(e).start()
    for e in range(1, tp):
        sum_turn(e).wait()
    total = ours[...]
    for e in range(1, tp):
        total = total + met[e]
    sums[...] = total


def copy_block(*refs):
    refs[-1][...] = refs[-2][...]


def pick_slots(sectioned, send_slot):
    slots, slab_rows, columns = sectioned.shape
    rows = min(128, slab_rows)
    return pl.pallas_call(
        copy_block,
        grid_spec=pltpu.PrefetchScalarGridSpec(
            num_scalar_prefetch=1,
            grid=(slots, slab_rows // rows),
            in_specs=[pl.BlockSpec((1, rows, columns), lambda i, r, slot: (slot[i], r, 0))],
            out_specs=pl.BlockSpec((1, rows, columns), lambda i, r, slot: (i, r, 0)),
        ),
        out_shape=jax.ShapeDtypeStruct(sectioned.shape, sectioned.dtype),
        name="pick_slots",
    )(send_slot, sectioned)


def settle(values):
    total, columns = values.shape
    rows = next(r for r in (32, 16, 8) if total % r == 0)
    return pl.pallas_call(
        copy_block,
        grid=(total // rows,),
        in_specs=[pl.BlockSpec((rows, columns), lambda i: (i, 0))],
        out_specs=pl.BlockSpec((rows, columns), lambda i: (i, 0)),
        out_shape=jax.ShapeDtypeStruct(values.shape, values.dtype),
        name="settle",
    )(values)


def per_device(sectioned, loader_owner, slab_order):
    owners = lax.axis_size("fsdp")
    tp = lax.axis_size("tp")
    myself = lax.axis_index("fsdp")
    slots, slab_rows, columns = sectioned.shape
    slab_count = loader_owner.shape[0]
    per_block = owners // tp
    slab_ids = jnp.arange(slab_count, dtype=jnp.int32)
    target = slab_ids // per_block % owners
    held = loader_owner == myself
    place = jnp.arange(owners, dtype=jnp.int32)
    picks = (target[None, :] == place[:, None]) & held[None, :]
    send_slot = jnp.sum(jnp.where(picks, slab_order[None, :], 0), axis=1)
    wanted = (place // per_block * owners + myself) * per_block + place % per_block
    sought = wanted[:, None] == slab_ids[None, :]
    from_owner = jnp.sum(jnp.where(sought, loader_owner[None, :], 0), axis=1)

    outgoing = pick_slots(sectioned, send_slot)
    rows = min(16, slab_rows)
    chunks = slab_rows // rows
    blocks = columns // BLOCK
    sizes = (owners, tp, chunks, rows, per_block, columns, 4)
    dma = pltpu.SemaphoreType.DMA
    anywhere = pl.BlockSpec(memory_space=pl.ANY)
    coded, scales, sums = pl.pallas_call(
        functools.partial(exchange, sizes),
        out_shape=(
            jax.ShapeDtypeStruct((per_block, slab_rows, tp * columns), jnp.bfloat16),
            jax.ShapeDtypeStruct((tp, per_block, slab_rows, LANES), jnp.float32),
            jax.ShapeDtypeStruct((rows, LANES), jnp.float32),
        ),
        in_specs=[pl.BlockSpec(memory_space=pltpu.SMEM), anywhere],
        out_specs=(anywhere, anywhere, pl.BlockSpec(memory_space=pltpu.VMEM)),
        scratch_shapes=[
            pltpu.VMEM((chunks, owners, rows, columns), jnp.bfloat16),
            pltpu.VMEM((2, tp, per_block, rows, columns), jnp.bfloat16),
            pltpu.VMEM((tp, per_block, slab_rows, LANES), jnp.float32),
            dma((chunks, owners)),
            dma((chunks, owners)),
            dma((chunks,)),
            dma((2, tp)),
            dma((chunks, tp)),
            dma((2,)),
            dma((2, tp)),
            dma((chunks, tp)),
            dma((2,)),
            pltpu.VMEM((rows, LANES), jnp.float32),
            pltpu.VMEM((rows, LANES), jnp.float32),
            pltpu.VMEM((owners, rows, LANES), jnp.float32),
            pltpu.VMEM((tp, rows, LANES), jnp.float32),
            dma((owners,)),
            dma((owners,)),
            dma((tp,)),
            dma((tp,)),
            pltpu.VMEM((owners, rows, columns), jnp.bfloat16),
        ],
        compiler_params=pltpu.CompilerParams(
            collective_id=0, has_side_effects=True, vmem_limit_bytes=56 * 1024 * 1024
        ),
        name="exchange",
    )(from_owner, outgoing)
    dequant = settle(coded.reshape(per_block * slab_rows, tp * columns))
    absmax = jnp.transpose(scales[..., :blocks], (1, 2, 0, 3)).reshape(-1, 256)
    offset = jnp.sum(sums) / float(slab_count * slab_rows * tp * blocks)
    centred = absmax - offset
    group_max = jnp.max(jnp.abs(centred), axis=1)
    scale_codes = centred / (group_max[:, None] + EPS)
    return (dequant, scale_codes, group_max)


def solution(mesh):
    return jax.shard_map(
        per_device,
        mesh=mesh,
        in_specs=(P("fsdp", None, "tp"), P(), P()),
        out_specs=(P(("tp", "fsdp"), None), P(("tp", "fsdp"), None), P(("tp", "fsdp"))),
        check_vma=False,
    )
```

time: 1360 us -> 696 us (0.51)
  Pallas kernels: 0 us -> 677 us
  waiting for transfers between devices: 588 us -> 0 us
  local copies, waits for them, and re-layouts: 257 us -> 2.19 us
  blocking collectives: 250 us -> 0 us
  other arithmetic: 244 us -> 5.98 us
  starting transfers between devices: 16.1 us -> 0 us
    pallas_call x0 -> x3, Pallas kernels: none -> 677 us  [the longest x1 629 us: per_device(): pl.pallas_call(functools.partial(exchange, sizes), out_shape=(jax.ShapeDt...]
    all_to_all x2 -> x0, waiting for transfers between devices: 588 us -> none  [the longest x1 588 us: per_device(): lax.all_to_all(outgoing, 'fsdp', split_axis=0, concat_axis=0, tiled=True)]
    psum x1 -> x0, blocking collectives: 250 us -> none  [per_device(): total = lax.psum(source_sum, ('tp', 'fsdp'))]
    convert_element_type x2 -> x0, other arithmetic: 115 us -> none  [the longest x1 88.9 us: hard_code(): coded = (spread * level).astype(jnp.bfloat16)]
    gather x7 -> x0, local copies, waits for them, and re-layouts: 86.4 us -> none  [the longest x3 42.9 us: per_device(): outgoing = jnp.take(sectioned, send_slot, axis=0)]
    unnamed x6 -> x4, local copies, waits for them, and re-layouts: 69.2 us -> 0.01 us
    abs x2 -> x0, other arithmetic: 52.4 us -> none  [block_absmax(): return jnp.max(jnp.abs(grouped), axis=-1)]
    abs x1 -> x0, local copies, waits for them, and re-layouts: 50 us -> none  [block_absmax(): return jnp.max(jnp.abs(grouped), axis=-1)]
  transfers between devices with their start and end apart: 2 -> 0, of which waited for: 1 -> 0; matrix products, arithmetic and copies ran while one was open for 6% -> 0% of each run, Pallas kernels for 0% -> 0%
where the time goes in v1:
time: 696 us; the launch traced here: 686 us
  Pallas kernels  677 us (97%)
    pallas_call x1, Pallas kernels, per_device(): pl.pallas_call(functools.partial(exchange, sizes), out_shape=(jax.ShapeDt...  629 us
    pallas_call x1, Pallas kernels, pick_slots(): pl.pallas_call(copy_block, grid_spec=pltpu.PrefetchScalarGridSpec(num_sca...  24.2 us
    pallas_call x1, Pallas kernels, settle(): pl.pallas_call(copy_block, grid=(total // rows,), in_specs=[pl.BlockSpec(...  23.6 us

profile of v1, /device:TPU:0, one launch (start us, length us, event | category | flops | bytes accessed | tf_op | source)
XLA Modules:
  0.0 686.1 jit_solution(7989841770264730887)
XLA Ops:
  0.6 0.7 broadcast_compare_fusion
  1.3 1.3 select_reduce_fusion.1.from_owner
  2.7 1.3 select_reduce_fusion.refs_0_
  3.9 24.2 %pick_slots.1.outgoing = bf16[8,256,6656]{2,1,0:T(8,128)(2,1)} custom-call(s32[8]{0:T(128)} %select_reduce_fusion.refs_0_, bf16[8,256,6656]{2,1,0:T(8,128)(2,1)} %refs_1_.1), custom_call_target="tpu_custom_call" | custom-call | tf_op jit(solution)/shard_map/pick_slots/pallas_call | solution.py:253
  28.2 628.8 %exchange.1 = (bf16[2,256,26624]{2,1,0:T(8,128)(2,1)}, f32[4,2,256,128]{3,2,1,0:T(8,128)}, f32[16,128]{1,0:T(8,128)}) custom-call(s32[8]{0:T(128)} %select_reduce_fusion.1.from_owner, bf16[8,256,6656]{2,1,0:T(8,128)(2,1)} %pick_slots.1.outgoing), custom_call_target="tpu_custom_call" | custom-call | tf_op jit(solution)/shard_map/exchange/pallas_call | solution.py:303
  656.9 1.3 reduce_sum.29
  658.9 0.0 copy-start
  658.9 23.6 %settle.1 = bf16[512,26624]{1,0:T(8,128)(2,1)} custom-call(bf16[512,26624]{1,0:T(8,128)(2,1)} %bitcast.3), custom_call_target="tpu_custom_call" | custom-call | tf_op jit(solution)/shard_map/settle/pallas_call | solution.py:269
  682.5 0.0 copy-done
  682.5 0.1 subtract_bitcast_fusion
  682.6 0.7 copy.7
  683.3 1.5 sub.27
  684.8 0.2 abs_reduce_fusion
  685.0 0.0 copy-start.1
  685.0 1.1 broadcast_divide_fusion
  686.1 0.0 copy-done.1
  (3 shorter events, 0.0 us)
Async XLA Ops:
  658.9 23.6 %copy-start = (f32[4,2,256,128]{3,2,1,0:T(8,128)S(1)}, f32[4,2,256,128]{3,2,1,0:T(8,128)}, u32[]{:S(2)}) copy-start(f32[4,2,256,128]{3,2,1,0:T(8,128)} %get-tuple-element.7) | copy-start | bytes 3145732
  685.0 1.1 copy-start.1
